TPU v7x, 32 devices: a whole 2x2x4 slice. The times are simulated.
32 devices in a mesh: section: 4 (over y, core), sim: 8 (over z, x).
Axes of the slice: x: 2, y: 2, z: 4, core: 2. Of those that a mesh axis runs over, the one named last changes fastest.
Arguments:
- state: float32 [128, 64, 8192], P('section', None, 'sim'), may hold values from -60 to 60
- owner: int32 [128, 1], P('section'), may hold values from 0 to 7; in each aligned block of 32 rows (0 to 31, 32 to 63, ...) at most 8 rows name the same one
- counts: int32 [128], P('section'), may hold values from 2048 to 8192
Outputs:
- slab_mean: float32 [128, 64], P('section')
- slab_cov: float32 [128, 4096], P('section', 'sim')
- group_cov: float32 [32, 4096], P(('section', 'sim'))
- global_mean: float32 [64], replicated
- global_cov: float32 [64, 64], replicated
Inputs may be any that keep to these rules, and one draw needn't show every extreme that they name: Among the 32 slabs of one group, no owner is named by more than 8 slabs, and one owner is named by exactly 8 slabs in some or all groups.
All inputs are finite; a program needn't handle non-finite values.
Results may differ from a plain program's by a relative error of at most 0.0003.
Values sent between devices are 32-bit elements; how exact they have to be, the bound alone decides.
A program may use at most 64 MiB of HBM per device.

v0:
```python
import jax
import jax.numpy as jnp
from jax import lax
from jax.sharding import PartitionSpec as P


def slot_payload(number, mean, comoment, capacity, n_sim, width):
    slot_cov = comoment / jnp.maximum(number - 1.0, 1.0)[:, None]
    cov_parts = slot_cov.reshape(capacity, n_sim, width * width // n_sim)
    mean_copies = jnp.broadcast_to(mean[:, None, :], (capacity, n_sim, width))
    return (cov_parts, mean_copies)


def owner_stats(number, mean, comoment):
    high = lax.Precision.HIGHEST
    width = mean.shape[1]
    group_count = jnp.sum(number)
    group_mean = jnp.sum(number[:, None] * mean, axis=0) / jnp.maximum(group_count, 1.0)
    offset = mean - group_mean[None, :]
    group_co = jnp.sum(comoment, axis=0) + jnp.einsum(
        "k,kv,kw->vw", number, offset, offset, precision=high
    ).reshape(width * width)
    return (group_count, group_mean, group_co)


def local(state, owner, counts):
    high = lax.Precision.HIGHEST
    slab_here, width, cells_dev = state.shape
    n_sim = lax.axis_size("sim")
    my_index = lax.axis_index("sim")
    capacity = 2 * slab_here // n_sim
    slots = n_sim * capacity
    target = owner[:, 0]
    order = jnp.arange(slab_here, dtype=jnp.int32)
    earlier = (target[:, None] == target[None, :]) & (order[None, :] < order[:, None])
    rank = jnp.sum(earlier.astype(jnp.int32), axis=1)
    slot_of = target * capacity + rank
    match = slot_of[:, None] == jnp.arange(slots, dtype=jnp.int32)[None, :]
    filled = jnp.any(match, axis=0)
    source_slab = jnp.sum(jnp.where(match, order[:, None], 0), axis=0)
    tile_start = my_index * cells_dev
    tile_count = jnp.clip(counts - tile_start, 0, cells_dev).astype(jnp.float32)
    live = jnp.arange(cells_dev, dtype=jnp.int32)[None, :] + tile_start < counts[:, None]
    tile_mean = (
        jnp.sum(jnp.where(live[:, None, :], state, 0.0), axis=2)
        / jnp.maximum(tile_count, 1.0)[:, None]
    )
    centered = jnp.where(live[:, None, :], state - tile_mean[:, :, None], 0.0)
    tile_co = jnp.einsum("svc,swc->svw", centered, centered, precision=high).reshape(
        slab_here, width * width
    )
    send_mean = jnp.where(filled[:, None], tile_mean[source_slab], 0.0).reshape(
        n_sim, capacity, width
    )
    send_co = jnp.where(filled[:, None], tile_co[source_slab], 0.0).reshape(
        n_sim, capacity, width * width
    )
    send_count = jnp.where(filled, tile_count[source_slab], 0.0).reshape(n_sim, capacity)
    means = lax.all_to_all(send_mean, "sim", split_axis=0, concat_axis=0, tiled=True)
    comoms = lax.all_to_all(send_co, "sim", split_axis=0, concat_axis=0, tiled=True)
    amounts = lax.all_to_all(send_count, "sim", split_axis=0, concat_axis=0, tiled=True)
    number = jnp.sum(amounts, axis=0)
    mean = jnp.sum(amounts[:, :, None] * means, axis=0) / jnp.maximum(number, 1.0)[:, None]
    offset = means - mean[None, :, :]
    extra = jnp.einsum("ik,ikv,ikw->kvw", amounts, offset, offset, precision=high)
    number, mean, comoment = (
        number,
        mean,
        jnp.sum(comoms, axis=0) + extra.reshape(number.shape[0], width * width),
    )
    cov_parts, mean_copies = slot_payload(number, mean, comoment, capacity, n_sim, width)
    back_cov, back_mean = (
        lax.all_to_all(cov_parts, "sim", split_axis=1, concat_axis=0, tiled=True),
        lax.all_to_all(mean_copies, "sim", split_axis=1, concat_axis=0, tiled=True),
    )
    slab_cov = back_cov[slot_of, 0]
    slab_mean = back_mean[slot_of, 0]
    group_count, group_mean, group_co = owner_stats(number, mean, comoment)
    group_cov = (group_co / jnp.maximum(group_count - 1.0, 1.0))[None, :]
    total, weighted = lax.psum((group_count, group_count * group_mean), ("section", "sim"))
    global_mean = weighted / total
    gap = group_mean - global_mean
    spread = lax.psum(group_co + group_count * jnp.outer(gap, gap).reshape(-1), ("section", "sim"))
    global_cov = (spread / (total - 1.0)).reshape(width, width)
    return (slab_mean, slab_cov, group_cov, global_mean, global_cov)


def solution(mesh):
    return jax.shard_map(
        local,
        mesh=mesh,
        in_specs=(P("section", None, "sim"), P("section", None), P("section")),
        out_specs=(P("section", None), P("section", "sim"), P(("section", "sim"), None), P(), P()),
        check_vma=False,
    )
```

profile of v0, /device:TPU:0, one launch (start us, length us, event | category | flops | bytes accessed | tf_op | source)
XLA Modules:
  0.0 160.8 jit_solution(15916009984353185825)
XLA Ops:
  0.6 0.9 convert_reduce_fusion
  1.5 0.7 fusion.19
  2.2 0.1 fusion.10
  2.3 0.1 select_reduce_fusion.1
  2.4 0.7 broadcast_maximum_fusion.1
  3.1 0.8 gather_fusion
  3.9 0.7 select_n.56
  4.5 7.3 %all-to-all-start = ((f32[8,1,8]{2,1,0:T(1,128)}), f32[8,1,8]{2,1,0:T(1,128)S(1)}, u32[]{:S(2)}, u32[]{:S(2)}) async-start(f32[8,1,8]{2,1,0:T(1,128)} %bitcast.5), calls=%async_computation | async-start | bytes 8192 | tf_op jit(solution)/shard_map/all_to_all | solution.py:61
  11.8 0.1 broadcast_in_dim.63
  11.9 0.7 broadcast_compare_fusion
  12.7 4.1 %select_reduce_fusion = f32[32,64]{1,0:T(8,128)S(1)} fusion(f32[32,64,1024]{2,1,0:T(8,128)} %param.3, pred[32,1024]{1,0:T(8,128)(4,1)S(1)} %broadcast_compare_fusion), kind=kLoop, calls=%fused_computation.8 | loop fusion | flops 4192256 | bytes 8429568 | tf_op jit(solution)/shard_map/reduce_sum | solution.py:45
  16.8 0.1 broadcast_divide_fusion.2
  16.9 0.6 gather_fusion.1
  17.5 14.9 %fusion = f32[32,64,64]{2,1,0:T(8,128)S(1)} fusion(f32[32,64,1024]{2,1,0:T(8,128)} %param.3, f32[32,64]{1,0:T(8,128)S(1)} %broadcast_divide_fusion.2, pred[32,1024]{1,0:T(8,128)(4,1)S(1)} %broadcast_compare_fusion), kind=kOutput, calls=%fused_computation.5 | convolution fusion | flops 1614807040 | bytes 8953856 | tf_op jit(solution)/shard_map/svc,swc->svw/dot_general | solution.py:49
  32.4 0.1 bitcast_select_fusion.1
  32.5 0.7 reshape.244
  33.2 0.4 reshape.205
  33.5 0.9 gather_fusion.3
  34.5 6.0 %all-to-all-start.1 = ((f32[8,1,512]{2,1,0:T(1,128)}), f32[8,1,512]{2,1,0:T(1,128)S(1)}, u32[]{:S(2)}, u32[]{:S(2)}) async-start(f32[8,1,512]{2,1,0:T(1,128)} %reshape.244), calls=%async_computation.1 | async-start | bytes 32768 | tf_op jit(solution)/shard_map/all_to_all | solution.py:59
  40.5 0.6 fusion.22
  41.1 6.0 %all-to-all-done.1 = f32[8,1,512]{2,1,0:T(1,128)S(1)} async-done(((f32[8,1,512]{2,1,0:T(1,128)}), f32[8,1,512]{2,1,0:T(1,128)S(1)}, u32[]{:S(2)}, u32[]{:S(2)}) %all-to-all-start.1) | async-done | bytes 16416 | tf_op jit(solution)/shard_map/all_to_all | solution.py:59
  47.1 0.5 broadcast.202
  47.6 0.7 reduce.4
  48.3 0.1 reshape.245
  48.3 0.1 multiply_reduce_fusion
  48.4 0.1 multiply_reduce_fusion.1
  48.5 0.7 reshape.246
  49.2 3.3 %all-to-all-start.2 = ((f32[8,1,512]{2,1,0:T(1,128)}), f32[8,1,512]{2,1,0:T(1,128)S(1)}, u32[]{:S(2)}, u32[]{:S(2)}) async-start(f32[8,1,512]{2,1,0:T(1,128)} %reshape.246), calls=%async_computation.2 | async-start | bytes 32768 | tf_op jit(solution)/shard_map/all_to_all | solution.py:74
  52.6 1.1 bitcast_select_fusion
  53.7 5.4 %all-to-all-done.2 = f32[8,1,512]{2,1,0:T(1,128)S(1)} async-done(((f32[8,1,512]{2,1,0:T(1,128)}), f32[8,1,512]{2,1,0:T(1,128)S(1)}, u32[]{:S(2)}, u32[]{:S(2)}) %all-to-all-start.2) | async-done | bytes 16416 | tf_op jit(solution)/shard_map/all_to_all | solution.py:74
  59.1 3.6 %all-to-all-start.3 = ((f32[8,8,4096]{2,1,0:T(8,128)}), f32[8,8,4096]{2,1,0:T(8,128)S(1)}, u32[]{:S(2)}, u32[]{:S(2)}) async-start(f32[8,8,4096]{2,1,0:T(8,128)} %bitcast_select_fusion), calls=%async_computation.3 | async-start | bytes 2097152 | tf_op jit(solution)/shard_map/all_to_all | solution.py:60
  63.9 0.7 broadcast_multiply_fusion.1
  64.6 41.6 %all-reduce.1 = (f32[64]{0:T(128)S(1)}, f32[]{:T(128)}) all-reduce(f32[64]{0:T(128)S(1)} %get-tuple-element.11, f32[]{:T(128)} %get-tuple-element.5), channel_id=1, replica_groups=mesh['section'=4,'sim'=8] {'section','sim'}, use_global_device_ids=true, to_apply=%region_10.11 | all-reduce | flops 65 | bytes 520 | tf_op jit(solution)/shard_map/psum | solution.py:80
  106.8 1.2 fusion.23
  108.1 0.7 reduce.5
  108.8 0.1 reshape.247
  108.8 1.2 gather_fusion.2
  110.1 0.1 reduce_sum.98
  110.2 0.6 add_reduce_fusion
  110.8 0.1 reshape.206
  110.9 0.7 fusion.6
  111.7 5.3 %all-to-all-start.4 = ((f32[8,8,512]{2,0,1:T(8,128)}), f32[8,8,512]{2,0,1:T(8,128)S(1)}, u32[]{:S(2)}, u32[]{:S(2)}) async-start(f32[8,8,512]{2,0,1:T(8,128)} %fusion.6), calls=%async_computation.4 | async-start | bytes 262144 | tf_op jit(solution)/shard_map/all_to_all | solution.py:73
  117.0 1.0 multiply_add_fusion
  117.9 0.7 div.85
  118.7 40.0 %psum.23 = f32[4096]{0:T(1024)S(1)} all-reduce(f32[4096]{0:T(1024)S(1)} %add.82), channel_id=1, replica_groups=mesh['section'=4,'sim'=8] {'section','sim'}, use_global_device_ids=true, to_apply=%region_12.13 | all-reduce | flops 4096 | bytes 32768 | tf_op jit(solution)/shard_map/psum | solution.py:83
  158.7 0.7 reshape.207
  159.4 0.1 all_to_all.46
  159.6 1.2 gather_fusion.4
  (13 shorter events, 0.2 us)
Async XLA Ops:
  4.5 29.9 %all-to-all-start = ((f32[8,1,8]{2,1,0:T(1,128)}), f32[8,1,8]{2,1,0:T(1,128)S(1)}, u32[]{:S(2)}, u32[]{:S(2)}) async-start(f32[8,1,8]{2,1,0:T(1,128)} %bitcast.5), calls=%async_computation | async-start | bytes 8192 | tf_op jit(solution)/shard_map/all_to_all | solution.py:61
  34.5 12.6 %all-to-all-start.1 = ((f32[8,1,512]{2,1,0:T(1,128)}), f32[8,1,512]{2,1,0:T(1,128)S(1)}, u32[]{:S(2)}, u32[]{:S(2)}) async-start(f32[8,1,512]{2,1,0:T(1,128)} %reshape.244), calls=%async_computation.1 | async-start | bytes 32768 | tf_op jit(solution)/shard_map/all_to_all | solution.py:59
  49.2 9.9 %all-to-all-start.2 = ((f32[8,1,512]{2,1,0:T(1,128)}), f32[8,1,512]{2,1,0:T(1,128)S(1)}, u32[]{:S(2)}, u32[]{:S(2)}) async-start(f32[8,1,512]{2,1,0:T(1,128)} %reshape.246), calls=%async_computation.2 | async-start | bytes 32768 | tf_op jit(solution)/shard_map/all_to_all | solution.py:74
  59.1 51.0 %all-to-all-start.3 = ((f32[8,8,4096]{2,1,0:T(8,128)}), f32[8,8,4096]{2,1,0:T(8,128)S(1)}, u32[]{:S(2)}, u32[]{:S(2)}) async-start(f32[8,8,4096]{2,1,0:T(8,128)} %bitcast_select_fusion), calls=%async_computation.3 | async-start | bytes 2097152 | tf_op jit(solution)/shard_map/all_to_all | solution.py:60
  111.7 47.8 %all-to-all-start.4 = ((f32[8,8,512]{2,0,1:T(8,128)}), f32[8,8,512]{2,0,1:T(8,128)S(1)}, u32[]{:S(2)}, u32[]{:S(2)}) async-start(f32[8,8,512]{2,0,1:T(8,128)} %fusion.6), calls=%async_computation.4 | async-start | bytes 262144 | tf_op jit(solution)/shard_map/all_to_all | solution.py:73
where the time goes:
time: 162 us; the launch traced here: 161 us
  blocking collectives  81.6 us (50%)
  starting transfers between devices  25.5 us (16%)
  matrix products  16.5 us (10%)
  other arithmetic  13.4 us (8%)
  waiting for transfers between devices  11.3 us (7%)
  local copies, waits for them, and re-layouts  9.73 us (6%)
  between operations  2.71 us (2%)
    psum x1, blocking collectives, local(): lax.psum((group_count, group_count * group_mean), ('section', 'sim'))  41.6 us
    psum x1, blocking collectives, local(): lax.psum(group_co + group_count * jnp.outer(gap, gap).reshape(-1), ('sect...  40 us
    dot_general x1, matrix products, local(): jnp.einsum('svc,swc->svw', centered, centered, precision=high)  14.9 us
    all_to_all x1, starting transfers between devices, local(): lax.all_to_all(send_count, 'sim', split_axis=0, concat_axis=0, tiled=True)  7.28 us
    all_to_all x1, starting transfers between devices, local(): lax.all_to_all(send_mean, 'sim', split_axis=0, concat_axis=0, tiled=True)  6.01 us
    all_to_all x1, waiting for transfers between devices, local(): lax.all_to_all(send_mean, 'sim', split_axis=0, concat_axis=0, tiled=True)  5.96 us
    all_to_all x1, waiting for transfers between devices, local(): lax.all_to_all(mean_copies, 'sim', split_axis=1, concat_axis=0, tiled=True)  5.37 us
    all_to_all x1, starting transfers between devices, local(): lax.all_to_all(cov_parts, 'sim', split_axis=1, concat_axis=0, tiled=True)  5.31 us
  transfers between devices with their start and end apart: 5, of which 2 were waited for; matrix products, arithmetic and copies ran while one was open for 19% of the time, Pallas kernels for 0%

commit v1 on v0

--- a/solution.py
+++ b/solution.py
@@ -80,7 +80,9 @@
     total, weighted = lax.psum((group_count, group_count * group_mean), ("section", "sim"))
     global_mean = weighted / total
     gap = group_mean - global_mean
-    spread = lax.psum(group_co + group_count * jnp.outer(gap, gap).reshape(-1), ("section", "sim"))
+    spread = lax.psum(
+        lax.psum(group_co + group_count * jnp.outer(gap, gap).reshape(-1), "sim"), "section"
+    )
     global_cov = (spread / (total - 1.0)).reshape(width, width)
     return (slab_mean, slab_cov, group_cov, global_mean, global_cov)
 

time: 162 us -> 169 us (1.043)
  blocking collectives: 81.6 us -> 89.3 us
    psum x1 -> x2, blocking collectives: 40 us -> 47.7 us  [the longest x1 37.5 us: local(): lax.psum(group_co + group_count * jnp.outer(gap, gap).reshape(-1), 'sim')]
  transfers between devices with their start and end apart: 5 -> 5, of which waited for: 2 -> 2; matrix products, arithmetic and copies ran while one was open for 19% -> 18% of each run, Pallas kernels for 0% -> 0%
where the time goes in v1:
time: 169 us; the launch traced here: 168 us
  blocking collectives  89.3 us (53%)
  starting transfers between devices  25.5 us (15%)
  matrix products  16.5 us (10%)
  other arithmetic  13.4 us (8%)
  waiting for transfers between devices  11.3 us (7%)
  local copies, waits for them, and re-layouts  9.73 us (6%)
  between operations  2.71 us (2%)
    psum x1, blocking collectives, local(): lax.psum((group_count, group_count * group_mean), ('section', 'sim'))  41.6 us
    psum x1, blocking collectives, local(): lax.psum(group_co + group_count * jnp.outer(gap, gap).reshape(-1), 'sim')  37.5 us
    dot_general x1, matrix products, local(): jnp.einsum('svc,swc->svw', centered, centered, precision=high)  14.9 us
    psum x1, blocking collectives, local(): lax.psum(lax.psum(group_co + group_count * jnp.outer(gap, gap).reshape(-1...  10.1 us
    all_to_all x1, starting transfers between devices, local(): lax.all_to_all(send_count, 'sim', split_axis=0, concat_axis=0, tiled=True)  7.28 us
    all_to_all x1, starting transfers between devices, local(): lax.all_to_all(send_mean, 'sim', split_axis=0, concat_axis=0, tiled=True)  6.01 us
    all_to_all x1, waiting for transfers between devices, local(): lax.all_to_all(send_mean, 'sim', split_axis=0, concat_axis=0, tiled=True)  5.96 us
    all_to_all x1, waiting for transfers between devices, local(): lax.all_to_all(mean_copies, 'sim', split_axis=1, concat_axis=0, tiled=True)  5.37 us
  transfers between devices with their start and end apart: 5, of which 2 were waited for; matrix products, arithmetic and copies ran while one was open for 18% of the time, Pallas kernels for 0%

profile of v1, /device:TPU:0, one launch (start us, length us, event | category | flops | bytes accessed | tf_op | source)
XLA Modules:
  0.0 168.5 jit_solution(14658935564518423849)
XLA Ops:
  0.6 0.9 convert_reduce_fusion
  1.5 0.7 fusion.19
  2.2 0.1 fusion.10
  2.3 0.1 select_reduce_fusion.1
  2.4 0.7 broadcast_maximum_fusion.1
  3.1 0.8 gather_fusion
  3.9 0.7 select_n.56
  4.5 7.3 %all-to-all-start = ((f32[8,1,8]{2,1,0:T(1,128)}), f32[8,1,8]{2,1,0:T(1,128)S(1)}, u32[]{:S(2)}, u32[]{:S(2)}) async-start(f32[8,1,8]{2,1,0:T(1,128)} %bitcast.5), calls=%async_computation | async-start | bytes 8192 | tf_op jit(solution)/shard_map/all_to_all | solution.py:61
  11.8 0.1 broadcast_in_dim.63
  11.9 0.7 broadcast_compare_fusion
  12.7 4.1 %select_reduce_fusion = f32[32,64]{1,0:T(8,128)S(1)} fusion(f32[32,64,1024]{2,1,0:T(8,128)} %param.3, pred[32,1024]{1,0:T(8,128)(4,1)S(1)} %broadcast_compare_fusion), kind=kLoop, calls=%fused_computation.8 | loop fusion | flops 4192256 | bytes 8429568 | tf_op jit(solution)/shard_map/reduce_sum | solution.py:45
  16.8 0.1 broadcast_divide_fusion.2
  16.9 0.6 gather_fusion.1
  17.5 14.9 %fusion = f32[32,64,64]{2,1,0:T(8,128)S(1)} fusion(f32[32,64,1024]{2,1,0:T(8,128)} %param.3, f32[32,64]{1,0:T(8,128)S(1)} %broadcast_divide_fusion.2, pred[32,1024]{1,0:T(8,128)(4,1)S(1)} %broadcast_compare_fusion), kind=kOutput, calls=%fused_computation.5 | convolution fusion | flops 1614807040 | bytes 8953856 | tf_op jit(solution)/shard_map/svc,swc->svw/dot_general | solution.py:49
  32.4 0.1 bitcast_select_fusion.1
  32.5 0.7 reshape.244
  33.2 0.4 reshape.205
  33.5 0.9 gather_fusion.3
  34.5 6.0 %all-to-all-start.1 = ((f32[8,1,512]{2,1,0:T(1,128)}), f32[8,1,512]{2,1,0:T(1,128)S(1)}, u32[]{:S(2)}, u32[]{:S(2)}) async-start(f32[8,1,512]{2,1,0:T(1,128)} %reshape.244), calls=%async_computation.1 | async-start | bytes 32768 | tf_op jit(solution)/shard_map/all_to_all | solution.py:59
  40.5 0.6 fusion.22
  41.1 6.0 %all-to-all-done.1 = f32[8,1,512]{2,1,0:T(1,128)S(1)} async-done(((f32[8,1,512]{2,1,0:T(1,128)}), f32[8,1,512]{2,1,0:T(1,128)S(1)}, u32[]{:S(2)}, u32[]{:S(2)}) %all-to-all-start.1) | async-done | bytes 16416 | tf_op jit(solution)/shard_map/all_to_all | solution.py:59
  47.1 0.5 broadcast.202
  47.6 0.7 reduce.4
  48.3 0.1 multiply_reduce_fusion
  48.4 0.1 multiply_reduce_fusion.1
  48.5 0.7 reshape.246
  49.2 3.3 %all-to-all-start.2 = ((f32[8,1,512]{2,1,0:T(1,128)}), f32[8,1,512]{2,1,0:T(1,128)S(1)}, u32[]{:S(2)}, u32[]{:S(2)}) async-start(f32[8,1,512]{2,1,0:T(1,128)} %reshape.246), calls=%async_computation.2 | async-start | bytes 32768 | tf_op jit(solution)/shard_map/all_to_all | solution.py:74
  52.6 1.1 bitcast_select_fusion
  53.7 5.4 %all-to-all-done.2 = f32[8,1,512]{2,1,0:T(1,128)S(1)} async-done(((f32[8,1,512]{2,1,0:T(1,128)}), f32[8,1,512]{2,1,0:T(1,128)S(1)}, u32[]{:S(2)}, u32[]{:S(2)}) %all-to-all-start.2) | async-done | bytes 16416 | tf_op jit(solution)/shard_map/all_to_all | solution.py:74
  59.1 3.6 %all-to-all-start.3 = ((f32[8,8,4096]{2,1,0:T(8,128)}), f32[8,8,4096]{2,1,0:T(8,128)S(1)}, u32[]{:S(2)}, u32[]{:S(2)}) async-start(f32[8,8,4096]{2,1,0:T(8,128)} %bitcast_select_fusion), calls=%async_computation.3 | async-start | bytes 2097152 | tf_op jit(solution)/shard_map/all_to_all | solution.py:60
  63.9 0.7 broadcast_multiply_fusion.1
  64.6 41.6 %all-reduce.1 = (f32[64]{0:T(128)S(1)}, f32[]{:T(128)}) all-reduce(f32[64]{0:T(128)S(1)} %get-tuple-element.11, f32[]{:T(128)} %get-tuple-element.5), channel_id=1, replica_groups=mesh['section'=4,'sim'=8] {'section','sim'}, use_global_device_ids=true, to_apply=%region_10.11 | all-reduce | flops 65 | bytes 520 | tf_op jit(solution)/shard_map/psum | solution.py:80
  106.8 1.2 fusion.23
  108.1 0.7 reduce.5
  108.8 0.1 reshape.247
  108.8 1.2 gather_fusion.2
  110.1 0.1 reduce_sum.98
  110.2 0.6 add_reduce_fusion
  110.8 0.1 reshape.206
  110.9 0.7 fusion.6
  111.7 5.3 %all-to-all-start.4 = ((f32[8,8,512]{2,0,1:T(8,128)}), f32[8,8,512]{2,0,1:T(8,128)S(1)}, u32[]{:S(2)}, u32[]{:S(2)}) async-start(f32[8,8,512]{2,0,1:T(8,128)} %fusion.6), calls=%async_computation.4 | async-start | bytes 262144 | tf_op jit(solution)/shard_map/all_to_all | solution.py:73
  117.0 1.0 multiply_add_fusion
  118.0 37.5 %psum.30 = f32[4096]{0:T(1024)S(1)} all-reduce(f32[4096]{0:T(1024)S(1)} %add.84), channel_id=1, replica_groups=mesh['section'=4,'sim'=8] {'sim'}, use_global_device_ids=true, to_apply=%region_12.13 | all-reduce | flops 4096 | bytes 32768 | tf_op jit(solution)/shard_map/psum | solution.py:84
  155.6 10.1 %psum.31 = f32[4096]{0:T(1024)S(1)} all-reduce(f32[4096]{0:T(1024)S(1)} %psum.30), channel_id=1, replica_groups=mesh['section'=4,'sim'=8] {'section'}, use_global_device_ids=true, to_apply=%region_13.14 | all-reduce | flops 4096 | bytes 32768 | tf_op jit(solution)/shard_map/psum | solution.py:83
  165.7 0.7 div.85
  166.4 0.7 reshape.207
  167.1 0.1 all_to_all.46
  167.2 1.2 gather_fusion.4
  (14 shorter events, 0.3 us)
Async XLA Ops:
  4.5 29.9 %all-to-all-start = ((f32[8,1,8]{2,1,0:T(1,128)}), f32[8,1,8]{2,1,0:T(1,128)S(1)}, u32[]{:S(2)}, u32[]{:S(2)}) async-start(f32[8,1,8]{2,1,0:T(1,128)} %bitcast.5), calls=%async_computation | async-start | bytes 8192 | tf_op jit(solution)/shard_map/all_to_all | solution.py:61
  34.5 12.6 %all-to-all-start.1 = ((f32[8,1,512]{2,1,0:T(1,128)}), f32[8,1,512]{2,1,0:T(1,128)S(1)}, u32[]{:S(2)}, u32[]{:S(2)}) async-start(f32[8,1,512]{2,1,0:T(1,128)} %reshape.244), calls=%async_computation.1 | async-start | bytes 32768 | tf_op jit(solution)/shard_map/all_to_all | solution.py:59
  49.2 9.9 %all-to-all-start.2 = ((f32[8,1,512]{2,1,0:T(1,128)}), f32[8,1,512]{2,1,0:T(1,128)S(1)}, u32[]{:S(2)}, u32[]{:S(2)}) async-start(f32[8,1,512]{2,1,0:T(1,128)} %reshape.246), calls=%async_computation.2 | async-start | bytes 32768 | tf_op jit(solution)/shard_map/all_to_all | solution.py:74
  59.1 51.0 %all-to-all-start.3 = ((f32[8,8,4096]{2,1,0:T(8,128)}), f32[8,8,4096]{2,1,0:T(8,128)S(1)}, u32[]{:S(2)}, u32[]{:S(2)}) async-start(f32[8,8,4096]{2,1,0:T(8,128)} %bitcast_select_fusion), calls=%async_computation.3 | async-start | bytes 2097152 | tf_op jit(solution)/shard_map/all_to_all | solution.py:60
  111.7 55.4 %all-to-all-start.4 = ((f32[8,8,512]{2,0,1:T(8,128)}), f32[8,8,512]{2,0,1:T(8,128)S(1)}, u32[]{:S(2)}, u32[]{:S(2)}) async-start(f32[8,8,512]{2,0,1:T(8,128)} %fusion.6), calls=%async_computation.4 | async-start | bytes 262144 | tf_op jit(solution)/shard_map/all_to_all | solution.py:73
